TPU v7x, 32 devices: a whole 2x2x4 slice. The times are simulated.
32 devices in a mesh: gx: 4 (over y, x), gy: 4 (over z), gz: 2 (over core).
Axes of the slice: x: 2, y: 2, z: 4, core: 2. Of those that a mesh axis runs over, the one named last changes fastest.
Arguments:
- right_side: float32 [3, 32, 128, 256], P(None, 'gx', 'gy', 'gz'), may hold values from -6 to 6
- mass_coef: float32 [3, 32, 128, 256], P(None, 'gx', 'gy', 'gz'), may hold values from 0.3 to 3
- curl_coef: float32 [3, 32, 128, 256], P(None, 'gx', 'gy', 'gz'), may hold values from 0.5 to 5
Outputs:
- solution: float32 [3, 32, 128, 256], P(None, 'gx', 'gy', 'gz')
- residual: float32 [3, 32, 128, 256], P(None, 'gx', 'gy', 'gz')
All inputs are finite; a program needn't handle non-finite values.
Results may differ from a plain program's by a relative error of at most 0.0003.
Values sent between devices are 32-bit elements; how exact they have to be, the bound alone decides.
A program may use at most 64 MiB of HBM per device.

v0:
```python
import functools

import jax
import jax.numpy as jnp
from jax import lax
from jax.experimental import pallas as pl
from jax.experimental.pallas import tpu as pltpu
from jax.sharding import PartitionSpec as P

ITERS = 4
SHIFT = 1.5
PAD = 8
MESH = pl.DeviceIdType.MESH


def kernel(sizes, r_ref, m_ref, c_ref, x_out, res_out, V, E, C, ZV, ZE, CZ, MX, MZ, YS, YR, LS, LR,
           PH, S, G, BK, VL, RED, send, recv, csend, crecv, rsend, rrecv):
    nx, ny, nz = sizes
    total = nx * ny * nz
    _, X, Y, Z = r_ref.shape
    ix, iy, iz = (lax.axis_index(a) for a in ("gx", "gy", "gz"))
    rank = (ix * ny + iy) * nz + iz
    sides = ZV.shape[1]
    north = sides - 1
    Yh = Y + PAD
    YE = Y + 2 * PAD
    loc = pl.ds(PAD, Y)
    inx = pl.ds(1, X)

    def dev(dx, dy, dz):
        return (lax.rem(ix + dx + nx, nx), lax.rem(iy + dy + ny, ny), lax.rem(iz + dz + nz, nz))

    def ranked(i):
        return (i // (ny * nz), lax.rem(i // nz, ny), lax.rem(i, nz))

    barrier = pltpu.get_barrier_semaphore()

    @pl.loop(1, total)
    def _(o):
        pl.semaphore_signal(
            barrier, inc=1, device_id=ranked(lax.rem(rank + o, total)), device_id_type=MESH
        )

    lane = lax.broadcasted_iota(jnp.int32, (Y, Z), 1)
    row = lax.broadcasted_iota(jnp.int32, (Y, Z), 0)
    lane_h = lax.broadcasted_iota(jnp.int32, (Yh, Z), 1)
    pending = []

    def remote(src, dst, ss, rs, to):
        copy = pltpu.make_async_remote_copy(
            src_ref=src, dst_ref=dst, send_sem=ss, recv_sem=rs, device_id=to, device_id_type=MESH
        )
        copy.start()
        pending.append(copy)
        return copy

    def up_z(own, other):
        ln = lane if own.shape[0] == Y else lane_h
        return pltpu.roll(jnp.where(ln == 0, other, own), Z - 1, 1)

    def dn_z(own, other):
        ln = lane if own.shape[0] == Y else lane_h
        return pltpu.roll(jnp.where(ln == Z - 1, other, own), 1, 1)

    def to_row(col):
        n = col.shape[0]
        wide = jnp.broadcast_to(col, (n, Z))
        return jnp.sum(jnp.where(row[:n] == lane[:n], wide, 0.0), axis=0, keepdims=True)

    def to_col(line, n):
        wide = jnp.broadcast_to(line, (n, Z))
        col = jnp.sum(jnp.where(row[:n] == lane[:n], wide, 0.0), axis=1, keepdims=True)
        return jnp.broadcast_to(col, (n, Z))

    def stage(p, F, down_y):
        for c in range(3):
            YS[p, 0, c] = F[c, 1 : X + 1, PAD + Y - 1, :]
            YS[p, 1, c] = F[down_y[c], 1 : X + 1, PAD, :]
        LS[p, 0] = F[0, X, PAD : PAD + 1, :]
        LS[p, 1] = F[1, 1, PAD + Y - 1 : PAD + Y, :]
        LS[p, 2] = to_row(F[0, X, loc, :][:, 0:1])
        LS[p, 3] = to_row(F[2, 1, loc, :][:, Z - 1 : Z])
        LS[p, 4] = to_row(YS[p, 0, 1][:, 0:1])
        LS[p, 5] = to_row(YS[p, 1, 2][:, Z - 1 : Z])

    line_to = ((1, -1, 0), (-1, 1, 0), (1, 0, -1), (-1, 0, 1), (0, 1, -1), (0, -1, 1))

    def launch(p, F, ZB, down_x):
        def sem(n):
            return send.at[p, n], recv.at[p, n]

        out = [
            remote(F.at[pl.ds(0, 3), X, loc], F.at[pl.ds(0, 3), 0, loc], *sem(0), dev(1, 0, 0)),
            remote(
                F.at[pl.ds(down_x, 3), 1, loc], F.at[pl.ds(down_x, 3), X + 1, loc], *sem(1),
                dev(-1, 0, 0),
            ),
            remote(YS.at[p, 0], YR.at[p, 0], *sem(2), dev(0, 1, 0)),
            remote(YS.at[p, 1], YR.at[p, 1], *sem(3), dev(0, -1, 0)),
        ]
        for n in range(6):
            out.append(remote(LS.at[p, n], LR.at[p, n], *sem(4 + n), dev(*line_to[n])))
        for n in range(sides):
            out.append(
                remote(
                    F.at[:, inx, loc], ZB.at[n, :, inx, loc], *sem(10 + n),
                    dev(0, 0, 1 if n == 0 else -1),
                )
            )
        return out

    def land(p, F, ZB, down_y, copies):
        for copy in copies:
            copy.wait_recv()
        for c in range(3):
            F[c, 1 : X + 1, PAD - 1, :] = YR[p, 0, c]
            F[down_y[c], 1 : X + 1, PAD + Y, :] = YR[p, 1, c]
        F[0, 0, PAD + Y : PAD + Y + 1, :] = LR[p, 0]
        F[1, X + 1, PAD - 1 : PAD, :] = LR[p, 1]
        ZB[north, 0, 0, loc, :] = to_col(LR[p, 2], Y)
        ZB[0, 2, X + 1, loc, :] = to_col(LR[p, 3], Y)
        ZB[north, 1, 1 : X + 1, PAD - 1, :] = to_col(LR[p, 4], X)
        ZB[0, 2, 1 : X + 1, PAD + Y, :] = to_col(LR[p, 5], X)

    straight = (0, 1, 2)
    folded = (3, 0, 2)

    V0 = V.at[0]
    for c in range(3):
        V0[c, 1 : X + 1, PAD : PAD + Y, :] = r_ref[c]
        C[c, 1 : X + 1, PAD : PAD + Y, :] = c_ref[c]
    stage(0, V0, straight)
    YS[5, 0, 0] = m_ref[1, :, Y - 1, :]
    YS[5, 0, 1] = c_ref[0, :, Y - 1, :]
    YS[5, 0, 2] = c_ref[2, :, Y - 1, :]

    pl.semaphore_wait(barrier, total - 1)
    coefs = [
        remote(m_ref.at[0, X - 1], MX, csend.at[0], crecv.at[0], dev(1, 0, 0)),
        remote(
            c_ref.at[pl.ds(1, 2), X - 1], C.at[pl.ds(1, 2), 0, loc], csend.at[1], crecv.at[1],
            dev(1, 0, 0),
        ),
        remote(YS.at[5, 0], YR.at[5, 0], csend.at[2], crecv.at[2], dev(0, 1, 0)),
        remote(m_ref.at[2], MZ, csend.at[3], crecv.at[3], dev(0, 0, 1)),
        remote(c_ref.at[pl.ds(0, 2)], CZ, csend.at[4], crecv.at[4], dev(0, 0, 1)),
    ]
    moving = launch(0, V0, ZV.at[0], 0)

    for copy in coefs:
        copy.wait_recv()
    C[0, 1 : X + 1, PAD - 1, :] = YR[5, 0, 1]
    C[2, 1 : X + 1, PAD - 1, :] = YR[5, 0, 2]

    @pl.loop(0, X)
    def _(i):
        p = i + 1
        c0, c1, c2 = (C[c, p, loc, :] for c in range(3))
        c0z, c1z = dn_z(c0, CZ[0, i]), dn_z(c1, CZ[1, i])
        low = pl.ds(PAD - 1, Y)
        m0, m1, m2 = (m_ref[c, i] for c in range(3))
        E[0, p, loc, :] = 1.0 / (m0 + c1 + c1z + c2 + C[2, p, low, :])
        E[1, p, loc, :] = 1.0 / (m1 + c2 + C[2, i, loc, :] + c0 + c0z)
        E[2, p, loc, :] = 1.0 / (m2 + c0 + C[0, p, low, :] + c1 + C[1, i, loc, :])
        before = jnp.where(i == 0, MX[...], m_ref[0, jnp.maximum(i - 1, 0)])
        back = YR[5, 0, 0, pl.ds(i, 1), :]
        m1y = jnp.where(row == 0, jnp.broadcast_to(back, (Y, Z)), pltpu.roll(m1, 1, 0))
        E[3, p, loc, :] = 1.0 / (m0 + before + m1 + m1y + m2 + dn_z(m2, MZ[i]))

    stage(1, E, folded)
    e_moving = launch(1, E, ZE, 1)
    land(0, V0, ZV.at[0], straight, moving)
    land(1, E, ZE, folded, e_moving)

    moments = {}
    full = pl.ds(0, Yh)
    full_up = pl.ds(1, Yh)
    low = pl.ds(PAD - 1, Y)
    high = pl.ds(PAD + 1, Y)
    hi_full = pl.ds(PAD, Yh)

    def fold(values):
        return jnp.sum(values.reshape(Y // 8, 8, Z), axis=0)

    for k in range(ITERS):
        W, ZW = V.at[k], ZV.at[k]
        if k:
            land(k + 1, W, ZW, straight, moving)

        def scaled(p, _):
            for c in range(3):
                S[c, p] = W[c, p] * E[c, p]
            return 0

        lax.fori_loop(0, X + 2, scaled, 0)

        def nodal(p, _):
            r2 = W[2, p, hi_full, :]
            q = (
                (W[0, p - 1, hi_full, :] - W[0, p, hi_full, :])
                + (W[1, p, pl.ds(PAD - 1, Yh), :] - W[1, p, hi_full, :])
                + (dn_z(r2, ZW[0, 2, p, hi_full, :]) - r2)
            )
            PH[p] = q * E[3, p, hi_full, :]
            return 0

        lax.fori_loop(1, X + 2, nodal, 0)

        def sz(side, c, p, rows):
            return ZW[side, c, p, rows, :] * ZE[side, c, p, rows, :]

        def curl_faces(p):
            s0, s1, s2 = (S[c, p, full, :] for c in range(3))
            g2 = C[2, p, full, :] * ((S[1, p + 1, full, :] - s1) - (S[0, p, full_up, :] - s0))
            t0, t2 = S[0, p, loc, :], S[2, p, loc, :]
            g1 = C[1, p, loc, :] * (
                (up_z(t0, sz(north, 0, p, loc)) - t0) - (S[2, p + 1, loc, :] - t2)
            )
            G[1, p, loc, :] = g1
            G[2, p, full, :] = g2
            return s1, s2

        curl_faces(0)

        def faces(p, _):
            s1, s2 = curl_faces(p)
            G[0, p, full, :] = C[0, p, full, :] * (
                (S[2, p, full_up, :] - s2) - (up_z(s1, sz(north, 1, p, full)) - s1)
            )
            return 0

        lax.fori_loop(1, X + 1, faces, 0)

        def apply(p, acc):
            i = p - 1
            s0, s1, s2 = (S[c, p, loc, :] for c in range(3))
            z0, z1, z2 = (sz(0, c, p, loc) for c in range(3))
            g0z = CZ[0, i] * ((sz(0, 2, p, high) - z2) - (pltpu.roll(s1, Z - 1, 1) - z1))
            g1z = CZ[1, i] * ((pltpu.roll(s0, Z - 1, 1) - z0) - (sz(0, 2, p + 1, loc) - z2))
            g0, g1, g2 = (G[c, p, loc, :] for c in range(3))
            g0b, g1b = dn_z(g0, g0z), dn_z(g1, g1z)
            n0 = ZW[north, 0, p, loc, :]
            n1 = ZW[north, 1, p, loc, :]
            qz = (
                (ZW[north, 0, i, loc, :] - n0)
                + (ZW[north, 1, p, low, :] - n1)
                + (pltpu.roll(W[2, p, loc, :], 1, 1) - ZW[north, 2, p, loc, :])
            )
            here = PH[p, 0:Y, :]
            b0 = s0 + (PH[p + 1, 0:Y, :] - here)
            b1 = s1 + (PH[p, 1 : Y + 1, :] - here)
            b2 = s2 + (up_z(here, qz * ZE[north, 3, p, loc, :]) - here)
            b = (b0, b1, b2)
            a = (
                (g1b - g1) - (G[2, p, low, :] - g2),
                (G[2, i, loc, :] - g2) - (g0b - g0),
                (G[0, p, low, :] - g0) - (G[1, i, loc, :] - g1),
            )
            w = [W[c, p, loc, :] for c in range(3)]
            v = [a[c] + (m_ref[c, i] * b[c] - SHIFT * w[c]) for c in range(3)]
            for c in range(3):
                BK[k, c, i] = b[c]
                if k + 1 < ITERS:
                    V[k + 1, c, p, loc, :] = v[c]
                else:
                    VL[c, i] = v[c]
            new = [acc[0] + fold(w[0] * b0 + w[1] * b1 + w[2] * b2)]
            for j in range(k + 1):
                bj = b if j == k else [BK[j, c, i] for c in range(3)]
                new.append(acc[j + 1] + fold(v[0] * bj[0] + v[1] * bj[1] + v[2] * bj[2]))
            return tuple(new)

        zero = jnp.zeros((8, Z), jnp.float32)
        acc = lax.fori_loop(1, X + 1, apply, (zero,) * (k + 2))
        moments[(k, k)] = acc[0]
        for j in range(k + 1):
            moments[(k + 1, j)] = acc[j + 1]
        if k + 1 < ITERS:
            stage(k + 2, V.at[k + 1], straight)
            moving = launch(k + 2, V.at[k + 1], ZV.at[k + 1], 0)

    keys = sorted(moments)
    line_lane = lax.broadcasted_iota(jnp.int32, (1, Z), 1)
    packed = jnp.zeros((1, Z), jnp.float32)
    for n, key in enumerate(keys):
        part = jnp.sum(jnp.sum(moments[key], axis=0, keepdims=True), axis=1, keepdims=True)
        packed = jnp.where(line_lane == n, part, packed)
    RED[rank] = packed

    def share(to, slot_from, o):
        return pltpu.make_async_remote_copy(
            src_ref=RED.at[slot_from], dst_ref=RED.at[slot_from], send_sem=rsend.at[o],
            recv_sem=rrecv.at[slot_from], device_id=ranked(to), device_id_type=MESH,
        )

    @pl.loop(1, total)
    def _(o):
        share(lax.rem(rank + o, total), rank, o).start()

    @pl.loop(1, total)
    def _(o):
        source = lax.rem(rank + o, total)
        share(source, source, o).wait_recv()

    summed = lax.fori_loop(0, total, lambda i, t: t + RED[i], jnp.zeros((1, Z), jnp.float32))
    gram = {}
    for n, (i, j) in enumerate(keys):
        value = jnp.sum(jnp.where(line_lane == n, summed, 0.0), axis=1, keepdims=True)
        gram[(i, j)] = value
        gram[(j, i)] = value

    def quad(left, right, entry):
        out = None
        for i, a in enumerate(left):
            for j, b in enumerate(right):
                term = (a * b) * entry(i, j)
                out = term if out is None else out + term
        return out

    one = jnp.ones((1, 1), jnp.float32)
    none = jnp.zeros((1, 1), jnp.float32)
    rho, pi, xi = [one], [], []
    gamma_old = alpha_old = None
    for k in range(ITERS):
        gamma = quad(rho, rho, lambda i, j: gram[(i, j)])
        delta = quad(rho, rho, lambda i, j: gram[(i + 1, j)] + SHIFT * gram[(i, j)])
        if k == 0:
            alpha = gamma / delta
            pi = list(rho)
        else:
            beta = gamma / gamma_old
            alpha = gamma / (delta - beta * gamma / alpha_old)
            pi = [rho[n] + beta * (pi[n] if n < len(pi) else none) for n in range(k + 1)]
        xi = [(xi[n] if n < len(xi) else none) + alpha * pi[n] for n in range(k + 1)]
        rho = rho + [none]
        moved = [none] * (k + 2)
        for n in range(k + 1):
            moved[n] = moved[n] + SHIFT * pi[n]
            moved[n + 1] = moved[n + 1] + pi[n]
        rho = [rho[n] - alpha * moved[n] for n in range(k + 2)]
        gamma_old, alpha_old = gamma, alpha

    spread = [jnp.broadcast_to(t, (Y, Z)) for t in rho]
    xspread = [jnp.broadcast_to(t, (Y, Z)) for t in xi]

    @pl.loop(0, X)
    def _(i):
        for c in range(3):
            res = spread[ITERS] * VL[c, i]
            sol = None
            for n in reversed(range(ITERS)):
                res = res + spread[n] * V[n, c, i + 1, loc, :]
                term = xspread[n] * BK[n, c, i]
                sol = term if sol is None else sol + term
            x_out[c, i] = sol
            res_out[c, i] = res

    for copy in pending:
        copy.wait_send()

    @pl.loop(1, total)
    def _(o):
        share(lax.rem(rank + o, total), rank, o).wait_send()


def body(sizes, right_side, mass_coef, curl_coef):
    _, X, Y, Z = right_side.shape
    nx, ny, nz = sizes
    total = nx * ny * nz
    sides = 1 if nz == 2 else 2
    XE, YE, Yh = X + 2, Y + 2 * PAD, Y + PAD
    f32 = jnp.float32
    vmem = pl.BlockSpec(memory_space=pltpu.VMEM)
    phases = ITERS + 1
    dma = pltpu.SemaphoreType.DMA
    return pl.pallas_call(
        functools.partial(kernel, sizes),
        out_shape=[jax.ShapeDtypeStruct(right_side.shape, f32)] * 2,
        in_specs=[vmem] * 3,
        out_specs=[vmem] * 2,
        scratch_shapes=[
            pltpu.VMEM((ITERS, 3, XE, YE, Z), f32),
            pltpu.VMEM((4, XE, YE, Z), f32),
            pltpu.VMEM((3, XE, YE, Z), f32),
            pltpu.VMEM((ITERS, sides, 3, XE, YE, Z), f32),
            pltpu.VMEM((sides, 4, XE, YE, Z), f32),
            pltpu.VMEM((2, X, Y, Z), f32),
            pltpu.VMEM((Y, Z), f32),
            pltpu.VMEM((X, Y, Z), f32),
            pltpu.VMEM((phases + 1, 2, 3, X, Z), f32),
            pltpu.VMEM((phases + 1, 2, 3, X, Z), f32),
            pltpu.VMEM((phases, 6, 1, Z), f32),
            pltpu.VMEM((phases, 6, 1, Z), f32),
            pltpu.VMEM((XE, Yh, Z), f32),
            pltpu.VMEM((3, XE, YE, Z), f32),
            pltpu.VMEM((3, XE, YE, Z), f32),
            pltpu.VMEM((ITERS, 3, X, Y, Z), f32),
            pltpu.VMEM((3, X, Y, Z), f32),
            pltpu.VMEM((total, 1, Z), f32),
            dma((phases, 10 + sides)),
            dma((phases, 10 + sides)),
            dma((5,)),
            dma((5,)),
            dma((total,)),
            dma((total,)),
        ],
        compiler_params=pltpu.CompilerParams(
            collective_id=0, has_side_effects=True, vmem_limit_bytes=56 * 1024 * 1024
        ),
        name="relayed_cg",
    )(right_side, mass_coef, curl_coef)


def solution(mesh):
    sizes = tuple(mesh.shape[a] for a in ("gx", "gy", "gz"))
    spec = P(None, "gx", "gy", "gz")
    return jax.shard_map(
        functools.partial(body, sizes), mesh=mesh, in_specs=(spec,) * 3, out_specs=(spec, spec),
        check_vma=False,
    )
```

profile of v0, /device:TPU:0, one launch (start us, length us, event | category | flops | bytes accessed | tf_op | source)
XLA Modules:
  0.0 54.4 jit_solution(8806702955021220143)
XLA Ops:
  0.6 51.2 %relayed_cg.1 = (f32[3,8,32,128]{3,2,1,0:T(8,128)}, f32[3,8,32,128]{3,2,1,0:T(8,128)}) custom-call(f32[3,8,32,128]{3,2,1,0:T(8,128)} %r_ref.1, f32[3,8,32,128]{3,2,1,0:T(8,128)} %m_ref.1, f32[3,8,32,128]{3,2,1,0:T(8,128)} %c_ref.1), custom_call_target="tpu_custom_call" | custom-call | tf_op jit(solution)/shard_map/relayed_cg/pallas_call | solution.py:376
  51.8 0.0 copy-start
  51.8 1.8 %copy.7 = f32[3,8,32,128]{3,2,1,0:T(8,128)} copy(f32[3,8,32,128]{3,2,1,0:T(8,128)} %get-tuple-element.4) | data formatting | bytes 786432
  53.7 0.0 copy-done
  53.7 0.7 %copy.8 = f32[3,8,32,128]{3,2,1,0:T(8,128)} copy(f32[3,8,32,128]{3,2,1,0:T(8,128)S(1)} %copy-done) | data formatting | bytes 786432
Async XLA Ops:
  51.8 1.8 %copy-start = (f32[3,8,32,128]{3,2,1,0:T(8,128)S(1)}, f32[3,8,32,128]{3,2,1,0:T(8,128)}, u32[]{:S(2)}) copy-start(f32[3,8,32,128]{3,2,1,0:T(8,128)} %get-tuple-element.5) | copy-start | bytes 1179652
where the time goes:
time: 54.6 us; the launch traced here: 54.4 us
  Pallas kernels  51.2 us (94%)
  local copies, waits for them, and re-layouts  2.57 us (5%)
  between operations  0.65 us (1%)
    pallas_call x1, Pallas kernels, body(): pl.pallas_call(functools.partial(kernel, sizes), out_shape=[jax.ShapeDtyp...  51.2 us
    unnamed x4, local copies, waits for them, and re-layouts  2.57 us

commit v1 on v0

--- a/solution.py
+++ b/solution.py
@@ -8,13 +8,13 @@
 from jax.sharding import PartitionSpec as P
 
 ITERS = 4
-SHIFT = 1.5
+UNROLL = True
 PAD = 8
 MESH = pl.DeviceIdType.MESH
 
 
 def kernel(sizes, r_ref, m_ref, c_ref, x_out, res_out, V, E, C, ZV, ZE, CZ, MX, MZ, YS, YR, LS, LR,
-           PH, S, G, BK, VL, RED, send, recv, csend, crecv, rsend, rrecv):
+           PH, S, G, ST, WL, RED, send, recv, csend, crecv, rsend, rrecv):
     nx, ny, nz = sizes
     total = nx * ny * nz
     _, X, Y, Z = r_ref.shape
@@ -30,16 +30,16 @@
     def dev(dx, dy, dz):
         return (lax.rem(ix + dx + nx, nx), lax.rem(iy + dy + ny, ny), lax.rem(iz + dz + nz, nz))
 
-    def ranked(i):
-        return (i // (ny * nz), lax.rem(i // nz, ny), lax.rem(i, nz))
-
     barrier = pltpu.get_barrier_semaphore()
 
-    @pl.loop(1, total)
-    def _(o):
-        pl.semaphore_signal(
-            barrier, inc=1, device_id=ranked(lax.rem(rank + o, total)), device_id_type=MESH
-        )
+    xs = [lax.rem(ix + d, nx) for d in range(nx)]
+    ys = [lax.rem(iy + d, ny) for d in range(ny)]
+    zs = [lax.rem(iz + d, nz) for d in range(nz)]
+    others = [
+        (a, b, c) for a in range(nx) for b in range(ny) for c in range(nz) if a or b or c
+    ]
+    for a, b, c in others:
+        pl.semaphore_signal(barrier, inc=1, device_id=(xs[a], ys[b], zs[c]), device_id_type=MESH)
 
     lane = lax.broadcasted_iota(jnp.int32, (Y, Z), 1)
     row = lax.broadcasted_iota(jnp.int32, (Y, Z), 0)
@@ -152,7 +152,7 @@
     C[0, 1 : X + 1, PAD - 1, :] = YR[5, 0, 1]
     C[2, 1 : X + 1, PAD - 1, :] = YR[5, 0, 2]
 
-    @pl.loop(0, X)
+    @pl.loop(0, X, unroll=UNROLL)
     def _(i):
         p = i + 1
         c0, c1, c2 = (C[c, p, loc, :] for c in range(3))
@@ -172,7 +172,44 @@
     land(0, V0, ZV.at[0], straight, moving)
     land(1, E, ZE, folded, e_moving)
 
-    moments = {}
+    line_lane = lax.broadcasted_iota(jnp.int32, (1, Z), 1)
+
+    def share(k, n, slot):
+        a, b, c = others[n]
+        return pltpu.make_async_remote_copy(
+            src_ref=RED.at[k, slot], dst_ref=RED.at[k, slot], send_sem=rsend.at[k, n],
+            recv_sem=rrecv.at[k, slot], device_id=(xs[a], ys[b], zs[c]), device_id_type=MESH,
+        )
+
+    def start_sums(k, gamma, delta):
+        packed = jnp.zeros((1, Z), jnp.float32)
+        for n, value in enumerate((gamma, delta)):
+            part = jnp.sum(jnp.sum(value, axis=0, keepdims=True), axis=1, keepdims=True)
+            packed = jnp.where(line_lane == n, part, packed)
+        RED[k, rank] = packed
+        for n in range(len(others)):
+            share(k, n, rank).start()
+
+    def finish_sums(k):
+        for n, (a, b, c) in enumerate(others):
+            share(k, n, (xs[a] * ny + ys[b]) * nz + zs[c]).wait_recv()
+        rows = [RED[k, n] for n in range(total)]
+        while len(rows) > 1:
+            rows = [sum(rows[n + 1 : n + 2], rows[n]) for n in range(0, len(rows), 2)]
+        return [
+            jnp.sum(jnp.where(line_lane == n, rows[0], 0.0), axis=1, keepdims=True)
+            for n in range(2)
+        ]
+
+    gamma_old = alpha_old = None
+
+    def step(k):
+        gamma, delta = finish_sums(k)
+        if k == 0:
+            return gamma, gamma / delta, None
+        beta = gamma / gamma_old
+        return gamma, gamma / (delta - beta * gamma / alpha_old), beta
+
     full = pl.ds(0, Yh)
     full_up = pl.ds(1, Yh)
     low = pl.ds(PAD - 1, Y)
@@ -192,7 +229,7 @@
                 S[c, p] = W[c, p] * E[c, p]
             return 0
 
-        lax.fori_loop(0, X + 2, scaled, 0)
+        lax.fori_loop(0, X + 2, scaled, 0, unroll=UNROLL)
 
         def nodal(p, _):
             r2 = W[2, p, hi_full, :]
@@ -204,7 +241,7 @@
             PH[p] = q * E[3, p, hi_full, :]
             return 0
 
-        lax.fori_loop(1, X + 2, nodal, 0)
+        lax.fori_loop(1, X + 2, nodal, 0, unroll=UNROLL)
 
         def sz(side, c, p, rows):
             return ZW[side, c, p, rows, :] * ZE[side, c, p, rows, :]
@@ -229,7 +266,13 @@
             )
             return 0
 
-        lax.fori_loop(1, X + 1, faces, 0)
+        lax.fori_loop(1, X + 1, faces, 0, unroll=UNROLL)
+
+        if k:
+            gamma_old, alpha_old, beta = step(k - 1)
+            alpha = jnp.broadcast_to(alpha_old, (Y, Z))
+            if k > 1:
+                beta = jnp.broadcast_to(beta, (Y, Z))
 
         def apply(p, acc):
             i = p - 1
@@ -257,110 +300,63 @@
                 (G[0, p, low, :] - g0) - (G[1, i, loc, :] - g1),
             )
             w = [W[c, p, loc, :] for c in range(3)]
-            v = [a[c] + (m_ref[c, i] * b[c] - SHIFT * w[c]) for c in range(3)]
+            gamma, delta = acc
+            terms = [[], []]
             for c in range(3):
-                BK[k, c, i] = b[c]
+                n = a[c] + m_ref[c, i] * b[c]
+                if k == 0:
+                    res, pre, img = w[c], b[c], n
+                else:
+                    u = ST[0, c, i]
+                    prev = r_ref[c, i] if k == 1 else ST[6, c, i]
+                    zz, qq, ss, pp = n, b[c], w[c], u
+                    if k > 1:
+                        zz = zz + beta * ST[1, c, i]
+                        qq = qq + beta * ST[2, c, i]
+                        ss = ss + beta * ST[3, c, i]
+                        pp = pp + beta * ST[4, c, i]
+                    if k + 1 < ITERS:
+                        ST[1, c, i] = zz
+                        ST[2, c, i] = qq
+                    ST[3, c, i] = ss
+                    ST[4, c, i] = pp
+                    ST[5, c, i] = alpha * pp if k == 1 else ST[5, c, i] + alpha * pp
+                    res, pre, img = prev - alpha * ss, u - alpha * qq, w[c] - alpha * zz
+                    ST[6, c, i] = res
+                ST[0, c, i] = pre
                 if k + 1 < ITERS:
-                    V[k + 1, c, p, loc, :] = v[c]
+                    V[k + 1, c, p, loc, :] = img
                 else:
-                    VL[c, i] = v[c]
-            new = [acc[0] + fold(w[0] * b0 + w[1] * b1 + w[2] * b2)]
-            for j in range(k + 1):
-                bj = b if j == k else [BK[j, c, i] for c in range(3)]
-                new.append(acc[j + 1] + fold(v[0] * bj[0] + v[1] * bj[1] + v[2] * bj[2]))
-            return tuple(new)
+                    WL[c, i] = img
+                terms[0].append(res * pre)
+                terms[1].append(img * pre)
+            return (
+                gamma + fold(terms[0][0] + terms[0][1] + terms[0][2]),
+                delta + fold(terms[1][0] + terms[1][1] + terms[1][2]),
+            )
 
         zero = jnp.zeros((8, Z), jnp.float32)
-        acc = lax.fori_loop(1, X + 1, apply, (zero,) * (k + 2))
-        moments[(k, k)] = acc[0]
-        for j in range(k + 1):
-            moments[(k + 1, j)] = acc[j + 1]
+        gamma, delta = lax.fori_loop(1, X + 1, apply, (zero, zero), unroll=UNROLL)
         if k + 1 < ITERS:
             stage(k + 2, V.at[k + 1], straight)
             moving = launch(k + 2, V.at[k + 1], ZV.at[k + 1], 0)
-
-    keys = sorted(moments)
-    line_lane = lax.broadcasted_iota(jnp.int32, (1, Z), 1)
-    packed = jnp.zeros((1, Z), jnp.float32)
-    for n, key in enumerate(keys):
-        part = jnp.sum(jnp.sum(moments[key], axis=0, keepdims=True), axis=1, keepdims=True)
-        packed = jnp.where(line_lane == n, part, packed)
-    RED[rank] = packed
-
-    def share(to, slot_from, o):
-        return pltpu.make_async_remote_copy(
-            src_ref=RED.at[slot_from], dst_ref=RED.at[slot_from], send_sem=rsend.at[o],
-            recv_sem=rrecv.at[slot_from], device_id=ranked(to), device_id_type=MESH,
-        )
-
-    @pl.loop(1, total)
-    def _(o):
-        share(lax.rem(rank + o, total), rank, o).start()
-
-    @pl.loop(1, total)
-    def _(o):
-        source = lax.rem(rank + o, total)
-        share(source, source, o).wait_recv()
-
-    summed = lax.fori_loop(0, total, lambda i, t: t + RED[i], jnp.zeros((1, Z), jnp.float32))
-    gram = {}
-    for n, (i, j) in enumerate(keys):
-        value = jnp.sum(jnp.where(line_lane == n, summed, 0.0), axis=1, keepdims=True)
-        gram[(i, j)] = value
-        gram[(j, i)] = value
-
-    def quad(left, right, entry):
-        out = None
-        for i, a in enumerate(left):
-            for j, b in enumerate(right):
-                term = (a * b) * entry(i, j)
-                out = term if out is None else out + term
-        return out
-
-    one = jnp.ones((1, 1), jnp.float32)
-    none = jnp.zeros((1, 1), jnp.float32)
-    rho, pi, xi = [one], [], []
-    gamma_old = alpha_old = None
-    for k in range(ITERS):
-        gamma = quad(rho, rho, lambda i, j: gram[(i, j)])
-        delta = quad(rho, rho, lambda i, j: gram[(i + 1, j)] + SHIFT * gram[(i, j)])
-        if k == 0:
-            alpha = gamma / delta
-            pi = list(rho)
-        else:
-            beta = gamma / gamma_old
-            alpha = gamma / (delta - beta * gamma / alpha_old)
-            pi = [rho[n] + beta * (pi[n] if n < len(pi) else none) for n in range(k + 1)]
-        xi = [(xi[n] if n < len(xi) else none) + alpha * pi[n] for n in range(k + 1)]
-        rho = rho + [none]
-        moved = [none] * (k + 2)
-        for n in range(k + 1):
-            moved[n] = moved[n] + SHIFT * pi[n]
-            moved[n + 1] = moved[n + 1] + pi[n]
-        rho = [rho[n] - alpha * moved[n] for n in range(k + 2)]
-        gamma_old, alpha_old = gamma, alpha
-
-    spread = [jnp.broadcast_to(t, (Y, Z)) for t in rho]
-    xspread = [jnp.broadcast_to(t, (Y, Z)) for t in xi]
-
-    @pl.loop(0, X)
+        start_sums(k, gamma, delta)
+
+    _, alpha, beta = step(ITERS - 1)
+    alpha = jnp.broadcast_to(alpha, (Y, Z))
+    beta = jnp.broadcast_to(beta, (Y, Z))
+
+    @pl.loop(0, X, unroll=UNROLL)
     def _(i):
         for c in range(3):
-            res = spread[ITERS] * VL[c, i]
-            sol = None
-            for n in reversed(range(ITERS)):
-                res = res + spread[n] * V[n, c, i + 1, loc, :]
-                term = xspread[n] * BK[n, c, i]
-                sol = term if sol is None else sol + term
-            x_out[c, i] = sol
-            res_out[c, i] = res
+            x_out[c, i] = ST[5, c, i] + alpha * (ST[0, c, i] + beta * ST[4, c, i])
+            res_out[c, i] = ST[6, c, i] - alpha * (WL[c, i] + beta * ST[3, c, i])
 
     for copy in pending:
         copy.wait_send()
-
-    @pl.loop(1, total)
-    def _(o):
-        share(lax.rem(rank + o, total), rank, o).wait_send()
+    for k in range(ITERS):
+        for n in range(len(others)):
+            share(k, n, rank).wait_send()
 
 
 def body(sizes, right_side, mass_coef, curl_coef):
@@ -394,18 +390,18 @@
             pltpu.VMEM((XE, Yh, Z), f32),
             pltpu.VMEM((3, XE, YE, Z), f32),
             pltpu.VMEM((3, XE, YE, Z), f32),
-            pltpu.VMEM((ITERS, 3, X, Y, Z), f32),
+            pltpu.VMEM((7, 3, X, Y, Z), f32),
             pltpu.VMEM((3, X, Y, Z), f32),
-            pltpu.VMEM((total, 1, Z), f32),
+            pltpu.VMEM((ITERS, total, 1, Z), f32),
             dma((phases, 10 + sides)),
             dma((phases, 10 + sides)),
             dma((5,)),
             dma((5,)),
-            dma((total,)),
-            dma((total,)),
+            dma((ITERS, total)),
+            dma((ITERS, total)),
         ],
         compiler_params=pltpu.CompilerParams(
-            collective_id=0, has_side_effects=True, vmem_limit_bytes=56 * 1024 * 1024
+            collective_id=0, has_side_effects=True, vmem_limit_bytes=24 * 1024 * 1024
         ),
         name="relayed_cg",
     )(right_side, mass_coef, curl_coef)

time: 54.6 us -> 46.1 us (0.84)
  Pallas kernels: 51.2 us -> 40.8 us
  local copies, waits for them, and re-layouts: 2.57 us -> 4.47 us
    pallas_call x1, Pallas kernels: 51.2 us -> 40.8 us  [body(): pl.pallas_call(functools.partial(kernel, sizes), out_shape=[jax.ShapeDtyp...]
    unnamed x4 -> x8, local copies, waits for them, and re-layouts: 2.57 us -> 4.47 us
where the time goes in v1:
time: 46.1 us; the launch traced here: 45.9 us
  Pallas kernels  40.8 us (89%)
  local copies, waits for them, and re-layouts  4.47 us (10%)
  between operations  0.65 us (1%)
    pallas_call x1, Pallas kernels, body(): pl.pallas_call(functools.partial(kernel, sizes), out_shape=[jax.ShapeDtyp...  40.8 us
    unnamed x8, local copies, waits for them, and re-layouts  4.47 us

profile of v1, /device:TPU:0, one launch (start us, length us, event | category | flops | bytes accessed | tf_op | source)
XLA Modules:
  0.0 45.9 jit_solution(13382520723295490228)
XLA Ops:
  0.6 0.0 copy-start
  0.6 1.0 %copy-done = f32[3,8,32,128]{3,2,1,0:T(8,128)S(1)} copy-done((f32[3,8,32,128]{3,2,1,0:T(8,128)S(1)}, f32[3,8,32,128]{3,2,1,0:T(8,128)}, u32[]{:S(2)}) %copy-start) | copy-done | bytes 393240
  1.6 0.0 copy-start.1
  1.6 1.0 %copy-done.1 = f32[3,8,32,128]{3,2,1,0:T(8,128)S(1)} copy-done((f32[3,8,32,128]{3,2,1,0:T(8,128)S(1)}, f32[3,8,32,128]{3,2,1,0:T(8,128)}, u32[]{:S(2)}) %copy-start.1) | copy-done | bytes 393240
  2.6 0.0 copy-start.2
  2.6 1.0 %copy-done.2 = f32[3,8,32,128]{3,2,1,0:T(8,128)S(1)} copy-done((f32[3,8,32,128]{3,2,1,0:T(8,128)S(1)}, f32[3,8,32,128]{3,2,1,0:T(8,128)}, u32[]{:S(2)}) %copy-start.2) | copy-done | bytes 393240
  3.6 40.8 %relayed_cg.1 = (f32[3,8,32,128]{3,2,1,0:T(8,128)S(1)}, f32[3,8,32,128]{3,2,1,0:T(8,128)S(1)}) custom-call(f32[3,8,32,128]{3,2,1,0:T(8,128)S(1)} %copy-done, f32[3,8,32,128]{3,2,1,0:T(8,128)S(1)} %copy-done.1, f32[3,8,32,128]{3,2,1,0:T(8,128)S(1)} %copy-done.2), custom_call_target="tpu_custom_call" | custom-call | tf_op jit(solution)/shard_map/relayed_cg/pallas_call | solution.py:372
  44.4 0.7 %copy.7 = f32[3,8,32,128]{3,2,1,0:T(8,128)} copy(f32[3,8,32,128]{3,2,1,0:T(8,128)S(1)} %get-tuple-element.4) | data formatting | bytes 786432
  45.1 0.7 %copy.8 = f32[3,8,32,128]{3,2,1,0:T(8,128)} copy(f32[3,8,32,128]{3,2,1,0:T(8,128)S(1)} %get-tuple-element.5) | data formatting | bytes 786432
Async XLA Ops:
  0.6 1.0 %copy-start = (f32[3,8,32,128]{3,2,1,0:T(8,128)S(1)}, f32[3,8,32,128]{3,2,1,0:T(8,128)}, u32[]{:S(2)}) copy-start(f32[3,8,32,128]{3,2,1,0:T(8,128)} %r_ref.1) | copy-start | bytes 1179652
  1.6 1.0 %copy-start.1 = (f32[3,8,32,128]{3,2,1,0:T(8,128)S(1)}, f32[3,8,32,128]{3,2,1,0:T(8,128)}, u32[]{:S(2)}) copy-start(f32[3,8,32,128]{3,2,1,0:T(8,128)} %m_ref.1) | copy-start | bytes 1179652
  2.6 1.0 %copy-start.2 = (f32[3,8,32,128]{3,2,1,0:T(8,128)S(1)}, f32[3,8,32,128]{3,2,1,0:T(8,128)}, u32[]{:S(2)}) copy-start(f32[3,8,32,128]{3,2,1,0:T(8,128)} %c_ref.1) | copy-start | bytes 1179652

commit v2 on v1

--- a/solution.py
+++ b/solution.py
@@ -13,11 +13,12 @@
 MESH = pl.DeviceIdType.MESH
 
 
-def kernel(sizes, r_ref, m_ref, c_ref, x_out, res_out, V, E, C, ZV, ZE, CZ, MX, MZ, YS, YR, LS, LR,
-           PH, S, G, ST, WL, RED, send, recv, csend, crecv, rsend, rrecv):
+def kernel(sizes, r_hbm, m_hbm, c_hbm, x_out, res_out, V, E, C, ZV, ZE, CZ, MX, MZ, YS, YR, LS, LR,
+           PH, S, G, ST, WL, RED, send, recv, csend, crecv, rsend, rrecv,
+           m_ref, lsem):
     nx, ny, nz = sizes
     total = nx * ny * nz
-    _, X, Y, Z = r_ref.shape
+    _, X, Y, Z = m_ref.shape
     ix, iy, iz = (lax.axis_index(a) for a in ("gx", "gy", "gz"))
     rank = (ix * ny + iy) * nz + iz
     sides = ZV.shape[1]
@@ -30,6 +31,13 @@
     def dev(dx, dy, dz):
         return (lax.rem(ix + dx + nx, nx), lax.rem(iy + dy + ny, ny), lax.rem(iz + dz + nz, nz))
 
+    loads = [
+        pltpu.make_async_copy(m_hbm, m_ref, lsem.at[0]),
+        pltpu.make_async_copy(c_hbm, C.at[:, inx, loc], lsem.at[1]),
+        pltpu.make_async_copy(r_hbm, V.at[0, :, inx, loc], lsem.at[2]),
+    ]
+    for load in loads:
+        load.start()
     barrier = pltpu.get_barrier_semaphore()
 
     xs = [lax.rem(ix + d, nx) for d in range(nx)]
@@ -85,21 +93,15 @@
 
     line_to = ((1, -1, 0), (-1, 1, 0), (1, 0, -1), (-1, 0, 1), (0, 1, -1), (0, -1, 1))
 
-    def launch(p, F, ZB, down_x):
+    def launch(p, F, ZB, down_x, between=lambda: None):
         def sem(n):
             return send.at[p, n], recv.at[p, n]
 
-        out = [
-            remote(F.at[pl.ds(0, 3), X, loc], F.at[pl.ds(0, 3), 0, loc], *sem(0), dev(1, 0, 0)),
-            remote(
-                F.at[pl.ds(down_x, 3), 1, loc], F.at[pl.ds(down_x, 3), X + 1, loc], *sem(1),
-                dev(-1, 0, 0),
-            ),
-            remote(YS.at[p, 0], YR.at[p, 0], *sem(2), dev(0, 1, 0)),
-            remote(YS.at[p, 1], YR.at[p, 1], *sem(3), dev(0, -1, 0)),
-        ]
+        out = []
         for n in range(6):
             out.append(remote(LS.at[p, n], LR.at[p, n], *sem(4 + n), dev(*line_to[n])))
+        out.append(remote(YS.at[p, 0], YR.at[p, 0], *sem(2), dev(0, 1, 0)))
+        out.append(remote(YS.at[p, 1], YR.at[p, 1], *sem(3), dev(0, -1, 0)))
         for n in range(sides):
             out.append(
                 remote(
@@ -107,6 +109,16 @@
                     dev(0, 0, 1 if n == 0 else -1),
                 )
             )
+        between()
+        out.append(
+            remote(F.at[pl.ds(0, 3), X, loc], F.at[pl.ds(0, 3), 0, loc], *sem(0), dev(1, 0, 0))
+        )
+        out.append(
+            remote(
+                F.at[pl.ds(down_x, 3), 1, loc], F.at[pl.ds(down_x, 3), X + 1, loc], *sem(1),
+                dev(-1, 0, 0),
+            )
+        )
         return out
 
     def land(p, F, ZB, down_y, copies):
@@ -126,24 +138,23 @@
     folded = (3, 0, 2)
 
     V0 = V.at[0]
-    for c in range(3):
-        V0[c, 1 : X + 1, PAD : PAD + Y, :] = r_ref[c]
-        C[c, 1 : X + 1, PAD : PAD + Y, :] = c_ref[c]
+    for load in loads:
+        load.wait()
+    YS[5, 0, 0] = m_ref[1, :, Y - 1, :]
+    YS[5, 0, 1] = C[0, 1 : X + 1, PAD + Y - 1, :]
+    YS[5, 0, 2] = C[2, 1 : X + 1, PAD + Y - 1, :]
     stage(0, V0, straight)
-    YS[5, 0, 0] = m_ref[1, :, Y - 1, :]
-    YS[5, 0, 1] = c_ref[0, :, Y - 1, :]
-    YS[5, 0, 2] = c_ref[2, :, Y - 1, :]
 
     pl.semaphore_wait(barrier, total - 1)
     coefs = [
+        remote(YS.at[5, 0], YR.at[5, 0], csend.at[2], crecv.at[2], dev(0, 1, 0)),
+        remote(m_ref.at[2], MZ, csend.at[3], crecv.at[3], dev(0, 0, 1)),
+        remote(C.at[pl.ds(0, 2), inx, loc], CZ, csend.at[4], crecv.at[4], dev(0, 0, 1)),
         remote(m_ref.at[0, X - 1], MX, csend.at[0], crecv.at[0], dev(1, 0, 0)),
         remote(
-            c_ref.at[pl.ds(1, 2), X - 1], C.at[pl.ds(1, 2), 0, loc], csend.at[1], crecv.at[1],
+            C.at[pl.ds(1, 2), X, loc], C.at[pl.ds(1, 2), 0, loc], csend.at[1], crecv.at[1],
             dev(1, 0, 0),
         ),
-        remote(YS.at[5, 0], YR.at[5, 0], csend.at[2], crecv.at[2], dev(0, 1, 0)),
-        remote(m_ref.at[2], MZ, csend.at[3], crecv.at[3], dev(0, 0, 1)),
-        remote(c_ref.at[pl.ds(0, 2)], CZ, csend.at[4], crecv.at[4], dev(0, 0, 1)),
     ]
     moving = launch(0, V0, ZV.at[0], 0)
 
@@ -308,7 +319,7 @@
                     res, pre, img = w[c], b[c], n
                 else:
                     u = ST[0, c, i]
-                    prev = r_ref[c, i] if k == 1 else ST[6, c, i]
+                    prev = V[0, c, p, loc, :] if k == 1 else ST[6, c, i]
                     zz, qq, ss, pp = n, b[c], w[c], u
                     if k > 1:
                         zz = zz + beta * ST[1, c, i]
@@ -339,8 +350,11 @@
         gamma, delta = lax.fori_loop(1, X + 1, apply, (zero, zero), unroll=UNROLL)
         if k + 1 < ITERS:
             stage(k + 2, V.at[k + 1], straight)
-            moving = launch(k + 2, V.at[k + 1], ZV.at[k + 1], 0)
-        start_sums(k, gamma, delta)
+            moving = launch(
+                k + 2, V.at[k + 1], ZV.at[k + 1], 0, lambda: start_sums(k, gamma, delta)
+            )
+        else:
+            start_sums(k, gamma, delta)
 
     _, alpha, beta = step(ITERS - 1)
     alpha = jnp.broadcast_to(alpha, (Y, Z))
@@ -372,7 +386,7 @@
     return pl.pallas_call(
         functools.partial(kernel, sizes),
         out_shape=[jax.ShapeDtypeStruct(right_side.shape, f32)] * 2,
-        in_specs=[vmem] * 3,
+        in_specs=[pl.BlockSpec(memory_space=pltpu.HBM)] * 3,
         out_specs=[vmem] * 2,
         scratch_shapes=[
             pltpu.VMEM((ITERS, 3, XE, YE, Z), f32),
@@ -399,12 +413,14 @@
             dma((5,)),
             dma((ITERS, total)),
             dma((ITERS, total)),
+            pltpu.VMEM((3, X, Y, Z), f32),
+            dma((3,)),
         ],
         compiler_params=pltpu.CompilerParams(
             collective_id=0, has_side_effects=True, vmem_limit_bytes=24 * 1024 * 1024
         ),
         name="relayed_cg",
-    )(right_side, mass_coef, curl_coef)
+    )(*(pltpu.with_memory_space_constraint(a, pltpu.HBM) for a in (right_side, mass_coef, curl_coef)))
 
 
 def solution(mesh):

time: 46.1 us -> 42.9 us (0.931)
  local copies, waits for them, and re-layouts: 4.47 us -> 1.49 us
    unnamed x8 -> x2, local copies, waits for them, and re-layouts: 4.47 us -> 1.49 us
where the time goes in v2:
time: 42.9 us; the launch traced here: 42.7 us
  Pallas kernels  40.6 us (95%)
  local copies, waits for them, and re-layouts  1.49 us (3%)
  between operations  0.64 us (1%)
    pallas_call x1, Pallas kernels, body(): pl.pallas_call(functools.partial(kernel, sizes), out_shape=[jax.ShapeDtyp...  40.6 us
    unnamed x2, local copies, waits for them, and re-layouts  1.49 us

profile of v2, /device:TPU:0, one launch (start us, length us, event | category | flops | bytes accessed | tf_op | source)
XLA Modules:
  0.0 42.7 jit_solution(17457423030390944421)
XLA Ops:
  0.6 40.6 %relayed_cg.1 = (f32[3,8,32,128]{3,2,1,0:T(8,128)S(1)}, f32[3,8,32,128]{3,2,1,0:T(8,128)S(1)}) custom-call(f32[3,8,32,128]{3,2,1,0:T(8,128)} %r_hbm.1, f32[3,8,32,128]{3,2,1,0:T(8,128)} %m_hbm.1, f32[3,8,32,128]{3,2,1,0:T(8,128)} %c_hbm.1), custom_call_target="tpu_custom_call" | custom-call | tf_op jit(solution)/shard_map/relayed_cg/pallas_call | solution.py:386
  41.2 0.7 %copy.7 = f32[3,8,32,128]{3,2,1,0:T(8,128)} copy(f32[3,8,32,128]{3,2,1,0:T(8,128)S(1)} %get-tuple-element.4) | data formatting | bytes 786432
  42.0 0.7 %copy.8 = f32[3,8,32,128]{3,2,1,0:T(8,128)} copy(f32[3,8,32,128]{3,2,1,0:T(8,128)S(1)} %get-tuple-element.5) | data formatting | bytes 786432

commit v3 on v2

--- a/solution.py
+++ b/solution.py
@@ -181,7 +181,7 @@
     stage(1, E, folded)
     e_moving = launch(1, E, ZE, 1)
     land(0, V0, ZV.at[0], straight, moving)
-    land(1, E, ZE, folded, e_moving)
+    land(1, E, ZE, folded, e_moving[:-2])
 
     line_lane = lax.broadcasted_iota(jnp.int32, (1, Z), 1)
 
@@ -233,14 +233,14 @@
     for k in range(ITERS):
         W, ZW = V.at[k], ZV.at[k]
         if k:
-            land(k + 1, W, ZW, straight, moving)
+            land(k + 1, W, ZW, straight, moving[:-2])
 
         def scaled(p, _):
             for c in range(3):
                 S[c, p] = W[c, p] * E[c, p]
             return 0
 
-        lax.fori_loop(0, X + 2, scaled, 0, unroll=UNROLL)
+        lax.fori_loop(1, X + 1, scaled, 0, unroll=UNROLL)
 
         def nodal(p, _):
             r2 = W[2, p, hi_full, :]
@@ -252,7 +252,7 @@
             PH[p] = q * E[3, p, hi_full, :]
             return 0
 
-        lax.fori_loop(1, X + 2, nodal, 0, unroll=UNROLL)
+        lax.fori_loop(2, X + 1, nodal, 0, unroll=UNROLL)
 
         def sz(side, c, p, rows):
             return ZW[side, c, p, rows, :] * ZE[side, c, p, rows, :]
@@ -268,8 +268,6 @@
             G[2, p, full, :] = g2
             return s1, s2
 
-        curl_faces(0)
-
         def faces(p, _):
             s1, s2 = curl_faces(p)
             G[0, p, full, :] = C[0, p, full, :] * (
@@ -277,7 +275,16 @@
             )
             return 0
 
-        lax.fori_loop(1, X + 1, faces, 0, unroll=UNROLL)
+        lax.fori_loop(1, X, faces, 0, unroll=UNROLL)
+
+        for copy in (moving if k else e_moving)[-2:]:
+            copy.wait_recv()
+        for p in (0, X + 1):
+            scaled(p, 0)
+        for p in (1, X + 1):
+            nodal(p, 0)
+        curl_faces(0)
+        faces(X, 0)
 
         if k:
             gamma_old, alpha_old, beta = step(k - 1)

time: 42.9 us -> 42.7 us (level)
  no operation moved by 1% of the time
where the time goes in v3:
time: 42.7 us; the launch traced here: 42.6 us
  Pallas kernels  40.4 us (95%)
  local copies, waits for them, and re-layouts  1.49 us (3%)
  between operations  0.64 us (1%)
    pallas_call x1, Pallas kernels, body(): pl.pallas_call(functools.partial(kernel, sizes), out_shape=[jax.ShapeDtyp...  40.4 us
    unnamed x2, local copies, waits for them, and re-layouts  1.49 us

profile of v3, /device:TPU:0, one launch (start us, length us, event | category | flops | bytes accessed | tf_op | source)
XLA Modules:
  0.0 42.6 jit_solution(9816585749845989121)
XLA Ops:
  0.6 40.4 %relayed_cg.1 = (f32[3,8,32,128]{3,2,1,0:T(8,128)S(1)}, f32[3,8,32,128]{3,2,1,0:T(8,128)S(1)}) custom-call(f32[3,8,32,128]{3,2,1,0:T(8,128)} %r_hbm.1, f32[3,8,32,128]{3,2,1,0:T(8,128)} %m_hbm.1, f32[3,8,32,128]{3,2,1,0:T(8,128)} %c_hbm.1), custom_call_target="tpu_custom_call" | custom-call | tf_op jit(solution)/shard_map/relayed_cg/pallas_call | solution.py:393
  41.1 0.7 %copy.7 = f32[3,8,32,128]{3,2,1,0:T(8,128)} copy(f32[3,8,32,128]{3,2,1,0:T(8,128)S(1)} %get-tuple-element.4) | data formatting | bytes 786432
  41.8 0.7 %copy.8 = f32[3,8,32,128]{3,2,1,0:T(8,128)} copy(f32[3,8,32,128]{3,2,1,0:T(8,128)S(1)} %get-tuple-element.5) | data formatting | bytes 786432
